TPU v7x, 32 devices: a whole 2x2x4 slice. The times are simulated.
32 devices in a mesh: tile: 8 (over z, x), cls: 4 (over y, core).
Axes of the slice: x: 2, y: 2, z: 4, core: 2. Of those that a mesh axis runs over, the one named last changes fastest.
Arguments:
- concentration: float32 [64, 4, 16384], P('cls', None, 'tile'), may hold values from 0.05 to 2
- velocity: float32 [2, 4, 16384], P(None, None, 'tile'), may hold values from -0.3 to 0.3
- land_mask: int32 [16384], P('tile'), may hold values 0 or 1
- settling: float32 [64], P('cls'), may hold values from 0.01 to 0.3
- breakage_rate: float32 [64], replicated, may hold values from 0.02 to 0.3
- kernel_levels: int32 [64, 64], replicated, may hold values from 100 to 1000, as said below
- pair_target: int32 [64, 64], replicated, may hold values from 0 to 63, as said below
- fragment_weights: int32 [64, 64], replicated, may hold values from 1 to 16
Outputs:
- flocs: float32 [64, 4, 16384], P('cls', None, 'tile')
Inputs may be any that keep to these rules, and one draw needn't show every extreme that they name: `kernel_levels`: symmetric. `pair_target`: symmetric, and entry [i, j] is at least the larger of i and j.
All inputs are finite; a program needn't handle non-finite values. No bound on the sum of `land_mask` on one device may be relied on, other than what follows from the above.
Results may differ from a plain program's by a relative error of at most 0.0001.
Values sent between devices are 32-bit elements; how exact they have to be, the bound alone decides.
A program may use at most 64 MiB of HBM per device.

v0:
```python
import functools

import jax
import jax.numpy as jnp
from jax import lax
from jax.experimental import pallas as pl
from jax.experimental.pallas import tpu as pltpu
from jax.sharding import PartitionSpec as P

CY = 512
CX = 4
half_scale = 0.5e-05
STEP = 8
LANES = 128
SPLIT = 2
UNIT = CY // SPLIT


def split_pair(value, lane, total):
    high = value.astype(jnp.bfloat16).astype(jnp.float32)
    return jnp.where(lane < total, high, value - high).astype(jnp.bfloat16)


def quad_rows(total):
    return sum(STEP * (total - first) for first in range(0, total, STEP))


def build_tables(levels_ref, target_ref, weights_ref, rate_ref, quad_ref, lin_ref):
    total = levels_ref.shape[0]
    wide = 2 * total
    levels = levels_ref[...].astype(jnp.float32)
    levels = jnp.concatenate([levels, levels], 1)
    target = target_ref[...]
    target = jnp.concatenate([target, target], 1)
    row = lax.broadcasted_iota(jnp.int32, (total, wide), 0)
    lane = lax.broadcasted_iota(jnp.int32, (total, wide), 1)
    col = jnp.where(lane < total, lane, lane - total)
    twice = 2.0 * levels
    birth = jnp.where(col < row, twice, jnp.where(col == row, levels, 0.0))
    offset = 0
    for first in range(0, total, STEP):
        count = total - first
        rank = row[first:]
        for i in range(first, first + STEP):
            value = jnp.where(target[i : i + 1] == rank, birth[i : i + 1], 0.0)
            value = value - jnp.where(rank == i, twice[i : i + 1], 0.0)
            packed = split_pair(value, lane[first:], total)
            quad_ref[offset : offset + count, :wide] = packed
            quad_ref[offset : offset + count, wide:] = packed
            offset += count
    weights = weights_ref[...].astype(jnp.float32)
    weights = jnp.concatenate([weights, weights], 1)
    rate = rate_ref[...]
    rate = jnp.concatenate([rate, rate], 1)
    lower = jnp.where(row <= col, weights, 0.0)
    frag = lower / jnp.sum(lower, axis=0, keepdims=True)
    value = frag * rate - jnp.where(row == col, rate, 0.0)
    packed = split_pair(value, lane, total)
    lin_ref[:, :wide] = packed
    lin_ref[:, wide:] = packed


def react(now, quad_ref, lin_ref):
    total = now.shape[0]
    high = now.astype(jnp.bfloat16)
    low = (now - high.astype(jnp.float32)).astype(jnp.bfloat16)
    stack = jnp.concatenate([high, high, low, low], 0)
    lin = jnp.dot(lin_ref[...], stack, preferred_element_type=jnp.float32)
    gain = None
    offset = 0
    for first in range(0, total, STEP):
        count = total - first
        made = jnp.dot(
            quad_ref[offset : offset + STEP * count, :], stack, preferred_element_type=jnp.float32
        )
        part = made[:count] * now[first : first + 1]
        for r in range(1, STEP):
            part = part + made[r * count : (r + 1) * count] * now[first + r : first + r + 1]
        gain = part if gain is None else jnp.concatenate([gain[:first], gain[first:] + part], 0)
        offset += STEP * count
    return now + gain * half_scale + lin


MESH = pl.DeviceIdType.MESH


def step_kernel(
    tiles,
    peers,
    flat_hbm,
    speed_hbm,
    water_hbm,
    settling_hbm,
    rate_hbm,
    levels_hbm,
    target_hbm,
    weights_hbm,
    out_ref,
    flat_ref,
    speed_ref,
    water_ref,
    settling_ref,
    rate_ref,
    levels_ref,
    target_ref,
    weights_ref,
    quad_ref,
    lin_ref,
    field_ref,
    moved_ref,
    whole_ref,
    done_ref,
    back_ref,
    load_sem,
    halo_send,
    halo_recv,
    out_send,
    out_recv,
    back_send,
    back_recv,
):
    layers, group, columns = moved_ref.shape
    tile_lanes = columns // LANES
    own = layers // peers
    base = layers * group
    tile = lax.axis_index("tile")
    me = lax.axis_index("cls")
    has_west = tile > 0
    has_east = tile < tiles - 1

    if peers == 4:
        partners = [lax.rem(me + 2, 4), 3 - me, me + 1 - 2 * lax.rem(me, 2)]
    else:
        partners = [lax.rem(me + d, peers) for d in range(1, peers)]

    barrier = pltpu.get_barrier_semaphore()

    @pl.when(has_west)
    def _():
        pl.semaphore_signal(barrier, inc=1, device_id={"tile": tile - 1}, device_id_type=MESH)

    @pl.when(has_east)
    def _():
        pl.semaphore_signal(barrier, inc=1, device_id={"tile": tile + 1}, device_id_type=MESH)

    for p in partners:
        pl.semaphore_signal(barrier, inc=1, device_id={"cls": p}, device_id_type=MESH)

    loads = [
        pltpu.make_async_copy(source, place, load_sem.at[n])
        for n, (source, place) in enumerate(
            (
                (flat_hbm, flat_ref),
                (speed_hbm, speed_ref),
                (water_hbm, water_ref),
                (settling_hbm, settling_ref),
                (rate_hbm, rate_ref),
                (levels_hbm, levels_ref),
                (target_hbm, target_ref),
                (weights_hbm, weights_ref),
            )
        )
    ]
    for copy in loads:
        copy.start()

    def span(start, width):
        return pl.ds(pl.multiple_of(start, width), width)

    def cols(x):
        return span(x * CY, CY)

    def strip(l):
        return pl.ds(l * group, group)

    for side, there in ((0, has_west), (1, has_east)):

        @pl.when(jnp.logical_not(there))
        def _():
            field_ref[:, cols(side * (CX + 1))] = jnp.zeros((base + 2 * layers, CY), jnp.float32)

    for copy in loads[:4]:
      copy.wait()
    for l in range(layers):
        for j in range(tile_lanes):
            field_ref[strip(l), CY + j * LANES : CY + (j + 1) * LANES] = flat_ref[
                pl.ds(j * layers + l, group, stride=tile_lanes * layers), :
            ]
    inner = pl.ds(CY, columns)
    field_ref[base : base + layers, inner] = speed_ref[0]
    field_ref[base + layers : base + 2 * layers, inner] = jnp.broadcast_to(
        water_ref[...].astype(jnp.float32), (layers, columns)
    )

    before = lax.div(tile + tiles - 1, tiles)
    after = lax.div(2 * (tiles - 1) - tile, tiles)
    pl.semaphore_wait(barrier, peers - 1 + before + after)

    odd = lax.rem(tile, 2)
    near = 1 - odd
    far = odd
    first = near * (CX - 1)
    last = far * (CX - 1)

    def halo(side, way):
        return pltpu.make_async_remote_copy(
            src_ref=field_ref.at[:, cols(side * (CX - 1) + 1)],
            dst_ref=field_ref.at[:, cols((1 - side) * (CX + 1))],
            send_sem=halo_send.at[way],
            recv_sem=halo_recv.at[way],
            device_id={"tile": tile - 1 + 2 * side},
            device_id_type=MESH,
        )

    def there(side):
        return (1 - side) * tile + side * (tiles - 1 - tile) > 0

    @pl.when(there(near))
    def _():
        halo(near, 0).start()

    def forward(n, u, start, width, s):
        at = span(start, width)
        return pltpu.make_async_remote_copy(
            src_ref=moved_ref.at[partners[n] * own + s, :, at],
            dst_ref=whole_ref.at[s, span(me * group, group), at],
            send_sem=out_send,
            recv_sem=out_recv.at[u, s],
            device_id={"cls": partners[n]},
            device_id_type=MESH,
        )

    def backward(n, q, start, width, s):
        at = span(start, width)
        return pltpu.make_async_remote_copy(
            src_ref=done_ref.at[s, span(partners[n] * group, group), at],
            dst_ref=back_ref.at[me * own + s, :, at],
            send_sem=back_send,
            recv_sem=back_recv.at[q],
            device_id={"cls": partners[n]},
            device_id_type=MESH,
        )

    def await_all(ref, sem):
        pltpu.make_async_copy(ref, ref, sem).wait()

    square = (group, group)
    diagonal = lax.broadcasted_iota(jnp.int32, square, 0) == lax.broadcasted_iota(
        jnp.int32, square, 1
    )
    settle = jnp.sum(jnp.where(diagonal, settling_ref[...], 0.0), axis=1, keepdims=True)
    settle = jnp.broadcast_to(settle, (group, CY))

    def transport(u, x, pieces):
        at = cols(x + 1)
        u_of = pl.ds(base, layers)
        w_of = pl.ds(base + layers, layers)
        speed, water = field_ref[u_of, at], field_ref[w_of, at]
        face_low = 0.5 * (field_ref[u_of, cols(x)] + speed) * (field_ref[w_of, cols(x)] * water)
        face_high = (
            0.5 * (speed + field_ref[u_of, cols(x + 2)]) * (water * field_ref[w_of, cols(x + 2)])
        )
        v = speed_ref[1, :, cols(x)]
        lane = lax.broadcasted_iota(jnp.int32, v.shape, 1)
        side_high = 0.5 * (v + pltpu.roll(v, CY - 1, 1)) * (water * pltpu.roll(water, CY - 1, 1))
        side_high = jnp.where(lane == CY - 1, 0.0, side_high)
        side_low = pltpu.roll(side_high, 1, 1)
        up = jnp.maximum
        down = jnp.minimum
        centre = (
            1.0 - up(face_high, 0.0) + down(face_low, 0.0) - up(side_high, 0.0) + down(side_low, 0.0)
        )
        west = up(face_low, 0.0)
        east = -down(face_high, 0.0)
        south = up(side_low, 0.0)
        north = -down(side_high, 0.0)
        for l in range(layers):
            c = field_ref[strip(l), at]
            moved = (
                (centre[l : l + 1] - settle) * c
                + west[l : l + 1] * field_ref[strip(l), cols(x)]
                + east[l : l + 1] * field_ref[strip(l), cols(x + 2)]
                + south[l : l + 1] * pltpu.roll(c, 1, 1)
                + north[l : l + 1] * pltpu.roll(c, CY - 1, 1)
            )
            if l > 0:
                moved = moved + settle * field_ref[strip(l - 1), at]
            moved_ref[l, :, cols(x)] = moved
        width = CY // pieces
        for h in range(pieces):
            for s in range(own):
                for n in range(peers - 1):
                    forward(n, u + h, x * CY + h * width, width, s).start()
        for s in range(own):
            whole_ref[s, span(me * group, group), cols(x)] = moved_ref[me * own + s, :, cols(x)]

    for x in range(1, CX - 1):
        transport(x - 1, x, 1)

    for copy in loads[4:]:
      copy.wait()
    build_tables(levels_ref, target_ref, weights_ref, rate_ref, quad_ref, lin_ref)

    @pl.when(there(near))
    def _():
        halo(near, 0).wait_send()

    @pl.when(there(far))
    def _():
        halo(far, 1).start()

    def edge(side, way, u, x, pieces):
        @pl.when(there(side))
        def _():
            halo(side, way).wait_recv()

        transport(u, x, pieces)

    def unit(u, q, start, width):
        at = span(start, width)
        for s in range(own):
            await_all(whole_ref.at[s, pl.ds(0, (peers - 1) * group), at], out_recv.at[u, s])
            now = react(whole_ref[s, :, at], quad_ref, lin_ref)
            done_ref[s, :, at] = react(now, quad_ref, lin_ref)
            for n in range(peers - 1):
                backward(n, q, start, width, s).start()
            back_ref[me * own + s, :, at] = done_ref[s, span(me * group, group), at]

    rows = CX - 1

    def full(q, carry):
        @pl.when(q == NEAR_AT)
        def _():
            edge(near, 0, CX - 2, first, 1)

        @pl.when(q == FAR_AT)
        def _():
            edge(far, 1, CX - 1, last, SPLIT)

        a = lax.div(q, CX - 2)
        x = (1 - a) * (q + 1) + a * first
        unit(q, q, x * CY, CY)
        return carry

    lax.fori_loop(0, rows, full, 0)

    def piece(h, carry):
        unit(rows + h, rows, last * CY + h * UNIT, UNIT)
        return carry

    lax.fori_loop(0, SPLIT, piece, 0)

    @pl.when(there(far))
    def _():
        halo(far, 1).wait_send()

    def finish(q, x):
        await_all(back_ref.at[pl.ds(0, (peers - 1) * own), :, cols(x)], back_recv.at[q])
        for l in range(layers):
            for j in range(CY // LANES):
                at = (x * (CY // LANES) + j) * layers + l
                out_ref[pl.ds(at, group, stride=tile_lanes * layers), :] = back_ref[
                    l, :, span(x * CY + j * LANES, LANES)
                ]

    await_all(moved_ref.at[pl.ds(0, (peers - 1) * own)], out_send)
    for q in range(CX):
        finish(q, (*range(1, CX - 1), first, last)[q])
    await_all(done_ref.at[:, pl.ds(0, (peers - 1) * group), :], back_send)


NEAR_AT = 1
FAR_AT = 2


def body(
    tiles,
    peers,
    concentration,
    velocity,
    land_mask,
    settling,
    breakage_rate,
    kernel_levels,
    pair_target,
    fragment_weights,
):
    group, layers, columns = concentration.shape
    total = kernel_levels.shape[0]
    own = layers // peers
    flat = concentration.reshape(group, layers, columns // LANES, LANES)
    flat = jnp.transpose(flat, (0, 2, 1, 3)).reshape(-1, LANES)
    operands = (
        flat,
        velocity,
        land_mask.reshape(1, columns),
        settling.reshape(1, group),
        breakage_rate.reshape(1, total),
        kernel_levels,
        pair_target,
        fragment_weights,
    )
    dma = pltpu.SemaphoreType.DMA
    done = pl.pallas_call(
        functools.partial(step_kernel, tiles, peers),
        out_shape=pltpu.VMEM((group * layers * columns // LANES, LANES), jnp.float32),
        in_specs=[pl.BlockSpec(memory_space=pl.ANY)] * len(operands),
        out_specs=pl.BlockSpec(memory_space=pltpu.VMEM),
        scratch_shapes=[
            pltpu.VMEM(flat.shape, jnp.float32),
            *[pltpu.VMEM(x.shape, x.dtype) for x in operands[1:]],
            pltpu.VMEM((quad_rows(total), 4 * total), jnp.bfloat16),
            pltpu.VMEM((total, 4 * total), jnp.bfloat16),
            pltpu.VMEM((layers * (group + 2), columns + 2 * CY), jnp.float32),
            pltpu.VMEM((layers, group, columns), jnp.float32),
            pltpu.VMEM((own, total, columns), jnp.float32),
            pltpu.VMEM((own, total, columns), jnp.float32),
            pltpu.VMEM((layers, group, columns), jnp.float32),
            dma((len(operands),)),
            dma((2,)),
            dma((2,)),
            dma,
            dma((CX - 1 + SPLIT, own)),
            dma,
            dma((CX,)),
        ],
        compiler_params=pltpu.CompilerParams(collective_id=0, has_side_effects=True),
    )(*operands)
    done = done.reshape(group, columns // LANES, layers, LANES)
    return jnp.transpose(done, (0, 2, 1, 3)).reshape(group, layers, columns)


def solution(mesh):
    return jax.shard_map(
        functools.partial(body, mesh.shape["tile"], mesh.shape["cls"]),
        mesh=mesh,
        in_specs=(
            P("cls", None, "tile"),
            P(None, None, "tile"),
            P("tile"),
            P("cls"),
            P(),
            P(),
            P(),
            P(),
        ),
        out_specs=P("cls", None, "tile"),
        check_vma=False,
    )
```

profile of v0, /device:TPU:25, one launch (start us, length us, event | category | flops | bytes accessed | tf_op | source)
XLA Modules:
  0.0 21.7 jit_solution(8378406658606663131)
XLA Ops:
  0.0 20.9 %shard_map.82 = f32[1024,128]{1,0:T(8,128)S(1)} custom-call(f32[1024,128]{1,0:T(8,128)} %bitcast.14, f32[2,4,2048]{2,1,0:T(4,128)} %speed_hbm.1, s32[1,2048]{1,0:T(1,128)} %bitcast.15, f32[1,16]{1,0:T(1,128)} %bitcast.16, f32[1,64]{1,0:T(1,128)} %bitcast.17, s32[64,64]{1,0:T(8,128)} %levels_hbm.1, s32[64,64]{1,0:T(8,128)} %target_hbm.1, s32[64,64]{1,0:T(8,128)} %weights_hbm.1), custom_call_target="tpu_custom_call" | custom-call | tf_op jit(solution)/shard_map/pallas_call | solution.py:404
  20.9 0.8 %copy.12 = f32[16,4,2048]{2,1,0:T(4,128)} copy(f32[16,4,2048]{2,1,0:T(4,128)S(1)} %bitcast.13) | data formatting | bytes 1048576
where the time goes:
time: 21.9 us; the launch traced here: 21.7 us
  Pallas kernels  20.9 us (95%)
  local copies, waits for them, and re-layouts  0.8 us (4%)
    pallas_call x1, Pallas kernels, body(): pl.pallas_call(functools.partial(step_kernel, tiles, peers), out_shape=pl...  20.9 us
    unnamed x1, local copies, waits for them, and re-layouts  0.8 us

commit v1 on v0

v1 whole, which is shorter than its diff:
```python
import functools

import jax
import jax.numpy as jnp
from jax import lax
from jax.experimental import pallas as pl
from jax.experimental.pallas import tpu as pltpu
from jax.sharding import PartitionSpec as P

CY = 512
CX = 4
half_scale = 0.5e-05
STEP = 8
EDGE = 16
LANES = 128
SPLIT = 2
UNIT = CY // SPLIT


def split_pair(value, lane, total):
    high = value.astype(jnp.bfloat16).astype(jnp.float32)
    return jnp.where(lane < total, high, value - high).astype(jnp.bfloat16)


def halves(value):
    high = value.astype(jnp.bfloat16)
    return high, (value - high.astype(jnp.float32)).astype(jnp.bfloat16)


def pair_span(i):
    return STEP * (i // STEP + 1)


def quad_rows(total):
    return sum(STEP * (total - first) for first in range(EDGE, total, STEP)) + EDGE


def pair_rows():
    return sum(pair_span(i) for i in range(EDGE))


def build_tables(levels_ref, target_ref, weights_ref, rate_ref, quad_ref, pair_ref):
    total = levels_ref.shape[0]
    wide = 2 * total
    narrow = levels_ref[...].astype(jnp.float32)
    levels = jnp.concatenate([narrow, narrow], 1)
    target = target_ref[...]
    target = jnp.concatenate([target, target], 1)
    row = lax.broadcasted_iota(jnp.int32, (total, wide), 0)
    lane = lax.broadcasted_iota(jnp.int32, (total, wide), 1)
    col = jnp.where(lane < total, lane, lane - total)
    twice = 2.0 * levels
    birth = jnp.where(col < row, twice, jnp.where(col == row, levels, 0.0))

    def put(offset, value, lane):
        count = value.shape[0]
        packed = split_pair(value, lane, total)
        quad_ref[offset : offset + count, :wide] = packed
        quad_ref[offset : offset + count, wide:] = packed
        return offset + count

    offset = 0
    for first in range(EDGE, total, STEP):
        rank = row[first:]
        for i in range(first, first + STEP):
            value = jnp.where(target[i : i + 1] == rank, birth[i : i + 1], 0.0)
            value = value - jnp.where(rank == i, twice[i : i + 1], 0.0)
            offset = put(offset, value, lane[first:])
    put(offset, jnp.where(col[:EDGE] >= EDGE, twice[:EDGE], 0.0), lane[:EDGE])

    count = pair_rows()

    def flat(make):
        return jnp.concatenate([make(i, pair_span(i)) for i in range(EDGE)], 1)

    rank = lax.broadcasted_iota(jnp.int32, (total, count), 0)
    one = flat(lambda i, width: jnp.full((1, width), i, jnp.int32))
    other = flat(lambda i, width: lax.broadcasted_iota(jnp.int32, (1, width), 1))
    goal = flat(lambda i, width: target_ref[i : i + 1, :width])
    level = flat(lambda i, width: 2.0 * levels_ref[i : i + 1, :width].astype(jnp.float32))
    level = jnp.where(other <= one, level, 0.0)
    same = other == one
    value = jnp.where(rank == goal, jnp.where(same, 0.5 * level, level), 0.0)
    value = value - jnp.where(rank == one, level, 0.0)
    value = value - jnp.where(rank == other, jnp.where(same, 0.0, level), 0.0)
    square = (total, total)
    row = lax.broadcasted_iota(jnp.int32, square, 0)
    col = lax.broadcasted_iota(jnp.int32, square, 1)
    lower = jnp.where(row <= col, weights_ref[...].astype(jnp.float32), 0.0)
    frag = lower / jnp.sum(lower, axis=0, keepdims=True)
    rate = rate_ref[...]
    linear = (frag * rate - jnp.where(row == col, rate, 0.0)) * (1.0 / half_scale)
    high, low = halves(jnp.concatenate([value, linear], 1))
    pair_ref[:total] = high
    pair_ref[total:] = low


def react(now, quad_ref, pair_ref):
    total = now.shape[0]
    high, low = halves(now)
    stack = jnp.concatenate([high, high, low, low], 0)
    ahead = [now[: pair_span(i)] * now[i : i + 1] for i in range(EDGE)]
    high, low = halves(jnp.concatenate([*ahead, now], 0))

    def dot(table, value):
        return jnp.dot(table, value, preferred_element_type=jnp.float32)

    def made_of(offset, count):
        return dot(quad_ref[offset : offset + count, :], stack)

    gain = None
    offset = 0
    for first in range(EDGE, total, STEP):
        count = total - first
        made = made_of(offset, STEP * count)
        part = made[:count] * now[first : first + 1]
        for r in range(1, STEP):
            part = part + made[r * count : (r + 1) * count] * now[first + r : first + r + 1]
        skip = first - EDGE
        gain = part if gain is None else jnp.concatenate([gain[:skip], gain[skip:] + part], 0)
        offset += STEP * count
    loss = made_of(offset, EDGE) * now[:EDGE]
    both = dot(pair_ref[...], high)
    rest = both[:total] + both[total:] + dot(pair_ref[:total], low)
    return now + (rest + jnp.concatenate([-loss, gain], 0)) * half_scale


MESH = pl.DeviceIdType.MESH
LAND = 4.0


def step_kernel(
    tiles,
    peers,
    flat_hbm,
    speed_hbm,
    water_hbm,
    settling_hbm,
    rate_hbm,
    levels_hbm,
    target_hbm,
    weights_hbm,
    out_ref,
    flat_ref,
    speed_ref,
    water_ref,
    settling_ref,
    rate_ref,
    levels_ref,
    target_ref,
    weights_ref,
    quad_ref,
    pair_ref,
    field_ref,
    drift_ref,
    outer_ref,
    halo_ref,
    moved_ref,
    whole_ref,
    done_ref,
    back_ref,
    load_sem,
    drift_send,
    drift_recv,
    halo_send,
    halo_recv,
    out_send,
    out_recv,
    back_send,
    back_recv,
):
    layers, group, columns = moved_ref.shape
    tile_lanes = columns // LANES
    own = layers // peers
    tile = lax.axis_index("tile")
    me = lax.axis_index("cls")
    has_west = tile > 0
    has_east = tile < tiles - 1

    if peers == 4:
        partners = [lax.rem(me + 2, 4), 3 - me, me + 1 - 2 * lax.rem(me, 2)]
    else:
        partners = [lax.rem(me + d, peers) for d in range(1, peers)]

    barrier = pltpu.get_barrier_semaphore()

    @pl.when(has_west)
    def _():
        pl.semaphore_signal(barrier, inc=1, device_id={"tile": tile - 1}, device_id_type=MESH)

    @pl.when(has_east)
    def _():
        pl.semaphore_signal(barrier, inc=1, device_id={"tile": tile + 1}, device_id_type=MESH)

    for p in partners:
        pl.semaphore_signal(barrier, inc=1, device_id={"cls": p}, device_id_type=MESH)

    loads = [
        pltpu.make_async_copy(source, place, load_sem.at[n])
        for n, (source, place) in enumerate(
            (
                (flat_hbm, flat_ref),
                (speed_hbm, speed_ref),
                (water_hbm, water_ref),
                (settling_hbm, settling_ref),
                (rate_hbm, rate_ref),
                (levels_hbm, levels_ref),
                (target_hbm, target_ref),
                (weights_hbm, weights_ref),
            )
        )
    ]
    for copy in loads:
        copy.start()

    def span(start, width):
        return pl.ds(pl.multiple_of(start, width), width)

    def cols(x):
        return span(x * CY, CY)

    def strip(l):
        return pl.ds(l * group, group)

    for side, exists in ((0, has_west), (1, has_east)):

        @pl.when(jnp.logical_not(exists))
        def _():
            drift_ref[:, cols(side * (CX + 1))] = jnp.full((layers, CY), LAND, jnp.float32)

    for copy in loads[:4]:
      copy.wait()
    drift_ref[:, pl.ds(CY, columns)] = jnp.where(
        jnp.broadcast_to(water_ref[...], (layers, columns)) == 1, speed_ref[0], LAND
    )
    for l in range(layers):
        for j in range(tile_lanes):
            field_ref[strip(l), j * LANES : (j + 1) * LANES] = flat_ref[
                pl.ds(j * layers + l, group, stride=tile_lanes * layers), :
            ]

    before = lax.div(tile + tiles - 1, tiles)
    after = lax.div(2 * (tiles - 1) - tile, tiles)
    pl.semaphore_wait(barrier, peers - 1 + before + after)

    far_side = lax.rem(tile, 2)
    sides = (far_side, 1 - far_side)
    edges = [side * (CX - 1) for side in sides]

    def there(way):
        side = sides[way]
        return (1 - side) * tile + side * (tiles - 1 - tile) > 0

    def beyond(way):
        return {"tile": tile - 1 + 2 * sides[way]}

    def drift(way):
        side = sides[way]
        return pltpu.make_async_remote_copy(
            src_ref=drift_ref.at[:, cols(edges[way] + 1)],
            dst_ref=drift_ref.at[:, cols((1 - side) * (CX + 1))],
            send_sem=drift_send.at[way],
            recv_sem=drift_recv.at[way],
            device_id=beyond(way),
            device_id_type=MESH,
        )

    def halo(way, h):
        return pltpu.make_async_remote_copy(
            src_ref=field_ref.at[:, span(edges[way] * CY + h * UNIT, UNIT)],
            dst_ref=halo_ref.at[way, :, pl.ds(h * UNIT, UNIT)],
            send_sem=halo_send.at[way],
            recv_sem=halo_recv.at[way, h],
            device_id=beyond(way),
            device_id_type=MESH,
        )

    for way in range(2):

        @pl.when(there(way))
        def _():
            drift(way).start()

    for way in HALO_ORDER:

        @pl.when(there(way))
        def _():
            for h in range(SPLIT):
                halo(way, h).start()

    def await_all(ref, sem):
        pltpu.make_async_copy(ref, ref, sem).wait()

    def forward(n, u, start, width, s):
        at = span(start, width)
        return pltpu.make_async_remote_copy(
            src_ref=moved_ref.at[partners[n] * own + s, :, at],
            dst_ref=whole_ref.at[s, span(me * group, group), at],
            send_sem=out_send,
            recv_sem=out_recv.at[u, s],
            device_id={"cls": partners[n]},
            device_id_type=MESH,
        )

    def send(u, start, width):
        for s in range(own):
            for n in range(peers - 1):
                forward(n, u, start, width, s).start()
        at = span(start, width)
        for s in range(own):
            whole_ref[s, span(me * group, group), at] = moved_ref[me * own + s, :, at]

    def backward(n, u, start, width, s):
        at = span(start, width)
        return pltpu.make_async_remote_copy(
            src_ref=done_ref.at[s, span(partners[n] * group, group), at],
            dst_ref=back_ref.at[me * own + s, :, at],
            send_sem=back_send,
            recv_sem=back_recv.at[u],
            device_id={"cls": partners[n]},
            device_id_type=MESH,
        )

    square = (group, group)
    diagonal = lax.broadcasted_iota(jnp.int32, square, 0) == lax.broadcasted_iota(
        jnp.int32, square, 1
    )
    settle = jnp.sum(jnp.where(diagonal, settling_ref[...], 0.0), axis=1, keepdims=True)
    settle = jnp.broadcast_to(settle, (group, CY))

    def transport(x, way=None):
        def row(at):
            value = drift_ref[:, cols(at)]
            return value, jnp.where(value < 0.5 * LAND, 1.0, 0.0)

        speed, water = row(x + 1)
        speed_low, water_low = row(x)
        speed_high, water_high = row(x + 2)
        face_low = 0.5 * (speed_low + speed) * (water_low * water)
        face_high = 0.5 * (speed + speed_high) * (water * water_high)
        v = speed_ref[1, :, cols(x)]
        lane = lax.broadcasted_iota(jnp.int32, v.shape, 1)
        side_high = 0.5 * (v + pltpu.roll(v, CY - 1, 1)) * (water * pltpu.roll(water, CY - 1, 1))
        side_high = jnp.where(lane == CY - 1, 0.0, side_high)
        side_low = pltpu.roll(side_high, 1, 1)
        up = jnp.maximum
        down = jnp.minimum
        centre = (
            1.0 - up(face_high, 0.0) + down(face_low, 0.0) - up(side_high, 0.0) + down(side_low, 0.0)
        )
        west = up(face_low, 0.0)
        east = -down(face_high, 0.0)
        south = up(side_low, 0.0)
        north = -down(side_high, 0.0)
        if way is None:
            inner = ((west, x - 1), (east, x + 1))
        else:
            eastern = sides[way] == 1
            outer_ref[way] = jnp.where(eastern, east, west)
            inner = ((jnp.where(eastern, west, east), x + 1 - 2 * sides[way]),)
        for l in range(layers):
            c = field_ref[strip(l), cols(x)]
            moved = (
                (centre[l : l + 1] - settle) * c
                + south[l : l + 1] * pltpu.roll(c, 1, 1)
                + north[l : l + 1] * pltpu.roll(c, CY - 1, 1)
            )
            for factor, at in inner:
                moved = moved + factor[l : l + 1] * field_ref[strip(l), cols(at)]
            if l > 0:
                moved = moved + settle * field_ref[strip(l - 1), cols(x)]
            moved_ref[l, :, cols(x)] = moved

    rows = CX - 2

    def prepare(way):
        @pl.when(there(way))
        def _():
            with jax.named_scope(f'driftwait{way}'):
                drift(way).wait_recv()

        transport(edges[way], way)

    def close(way):
        for h in range(SPLIT):
            start = edges[way] * CY + h * UNIT

            @pl.when(there(way))
            def _():
                with jax.named_scope(f'halowait{way}'):
                    halo(way, h).wait_recv()
                at = pl.ds(h * UNIT, UNIT)
                for l in range(layers):
                    moved_ref[l, :, span(start, UNIT)] += (
                        outer_ref[way, l : l + 1, at] * halo_ref[way, strip(l), at]
                    )

            send((rows + way) * SPLIT + h, start, UNIT)

    for x in range(1, CX - 1):
        transport(x)
        for h in range(SPLIT):
            send((x - 1) * SPLIT + h, x * CY + h * UNIT, UNIT)

    for copy in loads[4:]:
      copy.wait()
    build_tables(levels_ref, target_ref, weights_ref, rate_ref, quad_ref, pair_ref)

    @pl.when(jnp.logical_not(there(0)))
    def _():
        prepare(0)
        close(0)

    def slot(k):
        return lax.div(k, SPLIT) + lax.div(k, CX * SPLIT - 1) * (SPLIT - 1)

    def unit(u, start, width):
        at = span(start, width)
        for s in range(own):
            await_all(whole_ref.at[s, pl.ds(0, (peers - 1) * group), at], out_recv.at[u, s])
            now = react(whole_ref[s, :, at], quad_ref, pair_ref)
            done_ref[s, :, at] = react(now, quad_ref, pair_ref)
            for n in range(peers - 1):
                backward(n, slot(u), start, width, s).start()
            back_ref[me * own + s, :, at] = done_ref[s, span(me * group, group), at]

    def step(k, carry):
        for at, way, act in ((PREP_A, 0, prepare), (CLOSE_A, 0, close)):

            @pl.when(jnp.logical_and(k == at, there(0)))
            def _():
                act(way)

        for at, way, act in ((PREP_B, 1, prepare), (CLOSE_B, 1, close)):

            @pl.when(k == at)
            def _():
                act(way)

        q = lax.div(k, SPLIT)
        outer = lax.div(q, rows)
        b = lax.rem(q, rows)
        x = (1 - outer) * (q + 1) + outer * ((1 - b) * edges[0] + b * edges[1])
        unit(k, x * CY + lax.rem(k, SPLIT) * UNIT, UNIT)
        return carry

    lax.fori_loop(0, CX * SPLIT, step, 0)

    for way in range(2):

        @pl.when(there(way))
        def _():
            drift(way).wait_send()
            await_all(halo_ref.at[way], halo_send.at[way])

    def finish(u, start, width):
        await_all(
            back_ref.at[pl.ds(0, (peers - 1) * own), :, span(start, width)], back_recv.at[u]
        )
        for l in range(layers):
            for j in range(width // LANES):
                at = (lax.div(start, LANES) + j) * layers + l
                out_ref[pl.ds(at, group, stride=tile_lanes * layers), :] = back_ref[
                    l, :, span(start + j * LANES, LANES)
                ]

    await_all(moved_ref.at[pl.ds(0, (peers - 1) * own)], out_send)
    for q in range(rows):
        finish(q, (q + 1) * CY, CY)
    finish(rows, edges[0] * CY, CY)
    for h in range(SPLIT):
        finish(rows + 1 + h, edges[1] * CY + h * UNIT, UNIT)
    await_all(done_ref.at[:, pl.ds(0, (peers - 1) * group), :], back_send)


PREP_A = 2
CLOSE_A = 2
PREP_B = 3
CLOSE_B = 3
HALO_ORDER = (0, 1)


def body(
    tiles,
    peers,
    concentration,
    velocity,
    land_mask,
    settling,
    breakage_rate,
    kernel_levels,
    pair_target,
    fragment_weights,
):
    group, layers, columns = concentration.shape
    total = kernel_levels.shape[0]
    own = layers // peers
    flat = concentration.reshape(group, layers, columns // LANES, LANES)
    flat = jnp.transpose(flat, (0, 2, 1, 3)).reshape(-1, LANES)
    operands = (
        flat,
        velocity,
        land_mask.reshape(1, columns),
        settling.reshape(1, group),
        breakage_rate.reshape(1, total),
        kernel_levels,
        pair_target,
        fragment_weights,
    )
    dma = pltpu.SemaphoreType.DMA
    done = pl.pallas_call(
        functools.partial(step_kernel, tiles, peers),
        out_shape=pltpu.VMEM((group * layers * columns // LANES, LANES), jnp.float32),
        in_specs=[pl.BlockSpec(memory_space=pl.ANY)] * len(operands),
        out_specs=pl.BlockSpec(memory_space=pltpu.VMEM),
        scratch_shapes=[
            pltpu.VMEM(flat.shape, jnp.float32),
            *[pltpu.VMEM(x.shape, x.dtype) for x in operands[1:]],
            pltpu.VMEM((quad_rows(total), 4 * total), jnp.bfloat16),
            pltpu.VMEM((2 * total, pair_rows() + total), jnp.bfloat16),
            pltpu.VMEM((layers * group, columns), jnp.float32),
            pltpu.VMEM((layers, columns + 2 * CY), jnp.float32),
            pltpu.VMEM((2, layers, CY), jnp.float32),
            pltpu.VMEM((2, layers * group, CY), jnp.float32),
            pltpu.VMEM((layers, group, columns), jnp.float32),
            pltpu.VMEM((own, total, columns), jnp.float32),
            pltpu.VMEM((own, total, columns), jnp.float32),
            pltpu.VMEM((layers, group, columns), jnp.float32),
            dma((len(operands),)),
            dma((2,)),
            dma((2,)),
            dma((2,)),
            dma((2, SPLIT)),
            dma,
            dma((CX * SPLIT, own)),
            dma,
            dma((CX - 1 + SPLIT,)),
        ],
        compiler_params=pltpu.CompilerParams(collective_id=0, has_side_effects=True),
    )(*operands)
    done = done.reshape(group, columns // LANES, layers, LANES)
    return jnp.transpose(done, (0, 2, 1, 3)).reshape(group, layers, columns)


def solution(mesh):
    return jax.shard_map(
        functools.partial(body, mesh.shape["tile"], mesh.shape["cls"]),
        mesh=mesh,
        in_specs=(
            P("cls", None, "tile"),
            P(None, None, "tile"),
            P("tile"),
            P("cls"),
            P(),
            P(),
            P(),
            P(),
        ),
        out_specs=P("cls", None, "tile"),
        check_vma=False,
    )
```

time: 21.9 us -> 18.6 us (0.85)
  Pallas kernels: 20.9 us -> 17.6 us
    pallas_call x1, Pallas kernels: 20.9 us -> 17.6 us  [body(): pl.pallas_call(functools.partial(step_kernel, tiles, peers), out_shape=pl...]
where the time goes in v1:
time: 18.6 us; the launch traced here: 18.4 us
  Pallas kernels  17.6 us (95%)
  local copies, waits for them, and re-layouts  0.8 us (4%)
    pallas_call x1, Pallas kernels, body(): pl.pallas_call(functools.partial(step_kernel, tiles, peers), out_shape=pl...  17.6 us
    unnamed x1, local copies, waits for them, and re-layouts  0.8 us

profile of v1, /device:TPU:25, one launch (start us, length us, event | category | flops | bytes accessed | tf_op | source)
XLA Modules:
  0.0 18.4 jit_solution(13042647295588699223)
XLA Ops:
  0.0 17.6 %shard_map.82 = f32[1024,128]{1,0:T(8,128)S(1)} custom-call(f32[1024,128]{1,0:T(8,128)} %bitcast.14, f32[2,4,2048]{2,1,0:T(4,128)} %speed_hbm.1, s32[1,2048]{1,0:T(1,128)} %bitcast.15, f32[1,16]{1,0:T(1,128)} %bitcast.16, f32[1,64]{1,0:T(1,128)} %bitcast.17, s32[64,64]{1,0:T(8,128)} %levels_hbm.1, s32[64,64]{1,0:T(8,128)} %target_hbm.1, s32[64,64]{1,0:T(8,128)} %weights_hbm.1), custom_call_target="tpu_custom_call" | custom-call | tf_op jit(solution)/shard_map/pallas_call | solution.py:511
  17.6 0.8 %copy.12 = f32[16,4,2048]{2,1,0:T(4,128)} copy(f32[16,4,2048]{2,1,0:T(4,128)S(1)} %bitcast.13) | data formatting | bytes 1048576

commit v2 on v1

--- a/solution.py
+++ b/solution.py
@@ -12,9 +12,11 @@
 half_scale = 0.5e-05
 STEP = 8
 EDGE = 16
+LARGEST = 448
 LANES = 128
 SPLIT = 2
 UNIT = CY // SPLIT
+UNITS = CX - 2 + 2 * SPLIT
 
 
 def split_pair(value, lane, total):
@@ -105,21 +107,30 @@
     def dot(table, value):
         return jnp.dot(table, value, preferred_element_type=jnp.float32)
 
-    def made_of(offset, count):
-        return dot(quad_ref[offset : offset + count, :], stack)
+    spans = [(first, STEP * (total - first)) for first in range(EDGE, total, STEP)] + [(None, EDGE)]
+    made = {}
+    offset = 0
+    while spans:
+        taken = [spans.pop(0)]
+        while spans and sum(count for _, count in taken) + spans[0][1] <= LARGEST:
+            taken.append(spans.pop(0))
+        count = sum(count for _, count in taken)
+        product = dot(quad_ref[offset : offset + count, :], stack)
+        offset += count
+        start = 0
+        for first, count in taken:
+            made[first] = product[start : start + count]
+            start += count
 
     gain = None
-    offset = 0
     for first in range(EDGE, total, STEP):
         count = total - first
-        made = made_of(offset, STEP * count)
-        part = made[:count] * now[first : first + 1]
+        part = made[first][:count] * now[first : first + 1]
         for r in range(1, STEP):
-            part = part + made[r * count : (r + 1) * count] * now[first + r : first + r + 1]
+            part = part + made[first][r * count : (r + 1) * count] * now[first + r : first + r + 1]
         skip = first - EDGE
         gain = part if gain is None else jnp.concatenate([gain[:skip], gain[skip:] + part], 0)
-        offset += STEP * count
-    loss = made_of(offset, EDGE) * now[:EDGE]
+    loss = made[None] * now[:EDGE]
     both = dot(pair_ref[...], high)
     rest = both[:total] + both[total:] + dot(pair_ref[:total], low)
     return now + (rest + jnp.concatenate([-loss, gain], 0)) * half_scale
@@ -146,9 +157,7 @@
     water_ref,
     settling_ref,
     rate_ref,
-    levels_ref,
-    target_ref,
-    weights_ref,
+    table_ref,
     quad_ref,
     pair_ref,
     field_ref,
@@ -160,17 +169,15 @@
     done_ref,
     back_ref,
     load_sem,
-    drift_send,
     drift_recv,
-    halo_send,
     halo_recv,
     out_send,
     out_recv,
-    back_send,
     back_recv,
 ):
     layers, group, columns = moved_ref.shape
     tile_lanes = columns // LANES
+    block = CY // LANES * layers
     own = layers // peers
     tile = lax.axis_index("tile")
     me = lax.axis_index("cls")
@@ -204,14 +211,13 @@
                 (water_hbm, water_ref),
                 (settling_hbm, settling_ref),
                 (rate_hbm, rate_ref),
-                (levels_hbm, levels_ref),
-                (target_hbm, target_ref),
-                (weights_hbm, weights_ref),
             )
         )
     ]
     for copy in loads:
         copy.start()
+    for n, source in enumerate((levels_hbm, target_hbm, weights_hbm)):
+        pltpu.make_async_copy(source, table_ref.at[n], load_sem.at[len(loads)]).start()
 
     def span(start, width):
         return pl.ds(pl.multiple_of(start, width), width)
@@ -229,19 +235,28 @@
             drift_ref[:, cols(side * (CX + 1))] = jnp.full((layers, CY), LAND, jnp.float32)
 
     for copy in loads[:4]:
-      copy.wait()
+        copy.wait()
     drift_ref[:, pl.ds(CY, columns)] = jnp.where(
         jnp.broadcast_to(water_ref[...], (layers, columns)) == 1, speed_ref[0], LAND
     )
-    for l in range(layers):
-        for j in range(tile_lanes):
-            field_ref[strip(l), j * LANES : (j + 1) * LANES] = flat_ref[
-                pl.ds(j * layers + l, group, stride=tile_lanes * layers), :
-            ]
-
-    before = lax.div(tile + tiles - 1, tiles)
-    after = lax.div(2 * (tiles - 1) - tile, tiles)
-    pl.semaphore_wait(barrier, peers - 1 + before + after)
+    square = (group, group)
+    diagonal = lax.broadcasted_iota(jnp.int32, square, 0) == lax.broadcasted_iota(
+        jnp.int32, square, 1
+    )
+    settle = jnp.sum(jnp.where(diagonal, settling_ref[...], 0.0), axis=1, keepdims=True)
+    settle = jnp.broadcast_to(settle, (group, CY))
+
+    def line_up(x):
+        for l in range(layers):
+            for j in range(CY // LANES):
+                field_ref[strip(l), x * CY + j * LANES : x * CY + (j + 1) * LANES] = flat_ref[
+                    pl.ds(x * block + j * layers + l, group, stride=tile_lanes * layers), :
+                ]
+
+    def enter():
+        before = lax.div(tile + tiles - 1, tiles)
+        after = lax.div(2 * (tiles - 1) - tile, tiles)
+        pl.semaphore_wait(barrier, peers - 1 + before + after)
 
     far_side = lax.rem(tile, 2)
     sides = (far_side, 1 - far_side)
@@ -250,6 +265,8 @@
     def there(way):
         side = sides[way]
         return (1 - side) * tile + side * (tiles - 1 - tile) > 0
+
+    lonely = 1 - lax.div(tile + tiles - 1, tiles) * lax.div(2 * (tiles - 1) - tile, tiles)
 
     def beyond(way):
         return {"tile": tile - 1 + 2 * sides[way]}
@@ -259,7 +276,7 @@
         return pltpu.make_async_remote_copy(
             src_ref=drift_ref.at[:, cols(edges[way] + 1)],
             dst_ref=drift_ref.at[:, cols((1 - side) * (CX + 1))],
-            send_sem=drift_send.at[way],
+            send_sem=load_sem.at[way],
             recv_sem=drift_recv.at[way],
             device_id=beyond(way),
             device_id_type=MESH,
@@ -269,27 +286,27 @@
         return pltpu.make_async_remote_copy(
             src_ref=field_ref.at[:, span(edges[way] * CY + h * UNIT, UNIT)],
             dst_ref=halo_ref.at[way, :, pl.ds(h * UNIT, UNIT)],
-            send_sem=halo_send.at[way],
+            send_sem=load_sem.at[2 + way],
             recv_sem=halo_recv.at[way, h],
             device_id=beyond(way),
             device_id_type=MESH,
         )
 
-    for way in range(2):
-
-        @pl.when(there(way))
-        def _():
-            drift(way).start()
-
-    for way in HALO_ORDER:
-
-        @pl.when(there(way))
-        def _():
-            for h in range(SPLIT):
-                halo(way, h).start()
+    def reach_out():
+        for way in range(2):
+
+            @pl.when(there(way))
+            def _():
+                drift(way).start()
+                for h in range(SPLIT):
+                    halo(way, h).start()
 
     def await_all(ref, sem):
         pltpu.make_async_copy(ref, ref, sem).wait()
+
+    def arrival(u):
+        inner = (u - SPLIT) // SPLIT + SPLIT
+        return u if u < SPLIT else inner if u < (CX - 1) * SPLIT else u - (CX - 2) * (SPLIT - 1)
 
     def forward(n, u, start, width, s):
         at = span(start, width)
@@ -297,7 +314,7 @@
             src_ref=moved_ref.at[partners[n] * own + s, :, at],
             dst_ref=whole_ref.at[s, span(me * group, group), at],
             send_sem=out_send,
-            recv_sem=out_recv.at[u, s],
+            recv_sem=out_recv.at[arrival(u), s],
             device_id={"cls": partners[n]},
             device_id_type=MESH,
         )
@@ -315,18 +332,11 @@
         return pltpu.make_async_remote_copy(
             src_ref=done_ref.at[s, span(partners[n] * group, group), at],
             dst_ref=back_ref.at[me * own + s, :, at],
-            send_sem=back_send,
+            send_sem=load_sem.at[4],
             recv_sem=back_recv.at[u],
             device_id={"cls": partners[n]},
             device_id_type=MESH,
         )
-
-    square = (group, group)
-    diagonal = lax.broadcasted_iota(jnp.int32, square, 0) == lax.broadcasted_iota(
-        jnp.int32, square, 1
-    )
-    settle = jnp.sum(jnp.where(diagonal, settling_ref[...], 0.0), axis=1, keepdims=True)
-    settle = jnp.broadcast_to(settle, (group, CY))
 
     def transport(x, way=None):
         def row(at):
@@ -381,81 +391,98 @@
 
         transport(edges[way], way)
 
-    def close(way):
-        for h in range(SPLIT):
-            start = edges[way] * CY + h * UNIT
-
-            @pl.when(there(way))
-            def _():
-                with jax.named_scope(f'halowait{way}'):
-                    halo(way, h).wait_recv()
-                at = pl.ds(h * UNIT, UNIT)
-                for l in range(layers):
-                    moved_ref[l, :, span(start, UNIT)] += (
-                        outer_ref[way, l : l + 1, at] * halo_ref[way, strip(l), at]
-                    )
-
-            send((rows + way) * SPLIT + h, start, UNIT)
-
-    for x in range(1, CX - 1):
-        transport(x)
+    def close(way, h):
+        start = edges[way] * CY + h * UNIT
+
+        @pl.when(there(way))
+        def _():
+            with jax.named_scope(f'halowait{way}'):
+                halo(way, h).wait_recv()
+            at = pl.ds(h * UNIT, UNIT)
+            for l in range(layers):
+                moved_ref[l, :, span(start, UNIT)] += (
+                    outer_ref[way, l : l + 1, at] * halo_ref[way, strip(l), at]
+                )
+
+        send((rows + way) * SPLIT + h, start, UNIT)
+
+    def send_row(x):
         for h in range(SPLIT):
             send((x - 1) * SPLIT + h, x * CY + h * UNIT, UNIT)
 
-    for copy in loads[4:]:
-      copy.wait()
-    build_tables(levels_ref, target_ref, weights_ref, rate_ref, quad_ref, pair_ref)
+    for x in range(CX):
+        line_up(x)
+    transport(1)
+    enter()
+    reach_out()
+    send_row(1)
+    for x in range(2, CX - 1):
+        transport(x)
+        send_row(x)
+
+    loads[4].wait()
+    await_all(table_ref, load_sem.at[len(loads)])
+    build_tables(table_ref.at[0], table_ref.at[1], table_ref.at[2], rate_ref, quad_ref, pair_ref)
 
     @pl.when(jnp.logical_not(there(0)))
     def _():
         prepare(0)
-        close(0)
+        for h in range(SPLIT):
+            close(0, h)
 
     def slot(k):
-        return lax.div(k, SPLIT) + lax.div(k, CX * SPLIT - 1) * (SPLIT - 1)
+        row = k // SPLIT
+        return 0 if row < CX - 2 else row - (CX - 3) + (k % SPLIT if row == CX - 1 else 0)
 
     def unit(u, start, width):
         at = span(start, width)
         for s in range(own):
-            await_all(whole_ref.at[s, pl.ds(0, (peers - 1) * group), at], out_recv.at[u, s])
+            await_all(whole_ref.at[s, pl.ds(0, (peers - 1) * group), at], out_recv.at[arrival(u), s])
             now = react(whole_ref[s, :, at], quad_ref, pair_ref)
             done_ref[s, :, at] = react(now, quad_ref, pair_ref)
+            back_ref[me * own + s, :, at] = done_ref[s, span(me * group, group), at]
+
+    def start_of(k):
+        q, h = divmod(k, SPLIT)
+        return (q + 1 if q < rows else edges[q - rows]) * CY + h * UNIT
+
+    def give_back(k):
+        for s in range(own):
             for n in range(peers - 1):
-                backward(n, slot(u), start, width, s).start()
-            back_ref[me * own + s, :, at] = done_ref[s, span(me * group, group), at]
-
-    def step(k, carry):
-        for at, way, act in ((PREP_A, 0, prepare), (CLOSE_A, 0, close)):
-
-            @pl.when(jnp.logical_and(k == at, there(0)))
+                backward(n, slot(k), start_of(k), UNIT, s).start()
+
+    def act(name):
+        kind, *rest = name
+        if kind == "unit":
+            k, wide = rest
+            unit(k, start_of(k), CY if wide else UNIT)
+        elif kind == "back":
+            give_back(rest[0])
+        elif kind == "far":
+            @pl.when(there(0))
             def _():
-                act(way)
-
-        for at, way, act in ((PREP_B, 1, prepare), (CLOSE_B, 1, close)):
-
-            @pl.when(k == at)
+                prepare(0) if rest[0] == "prep" else close(0, rest[0])
+        else:
+            @pl.when(lonely == (1 if kind == "alone" else 0))
             def _():
-                act(way)
-
-        q = lax.div(k, SPLIT)
-        outer = lax.div(q, rows)
-        b = lax.rem(q, rows)
-        x = (1 - outer) * (q + 1) + outer * ((1 - b) * edges[0] + b * edges[1])
-        unit(k, x * CY + lax.rem(k, SPLIT) * UNIT, UNIT)
-        return carry
-
-    lax.fori_loop(0, CX * SPLIT, step, 0)
+                prepare(1) if rest[0] == "prep" else close(1, rest[0])
+
+    for name in PLAN:
+        act(name)
 
     for way in range(2):
 
         @pl.when(there(way))
         def _():
             drift(way).wait_send()
-            await_all(halo_ref.at[way], halo_send.at[way])
+            await_all(halo_ref.at[way], load_sem.at[2 + way])
+
+    def ahead(start, width):
+        return pl.ds(pl.multiple_of(start, UNIT), width)
 
     def finish(u, start, width):
         await_all(
-            back_ref.at[pl.ds(0, (peers - 1) * own), :, span(start, width)], back_recv.at[u]
+            back_ref.at[pl.ds(0, (peers - 1) * own), :, ahead(start, width)], back_recv.at[u]
         )
         for l in range(layers):
             for j in range(width // LANES):
@@ -465,19 +492,38 @@
                 ]
 
     await_all(moved_ref.at[pl.ds(0, (peers - 1) * own)], out_send)
-    for q in range(rows):
-        finish(q, (q + 1) * CY, CY)
-    finish(rows, edges[0] * CY, CY)
+    finish(0, CY, rows * CY)
+    finish(1, edges[0] * CY, CY)
     for h in range(SPLIT):
-        finish(rows + 1 + h, edges[1] * CY + h * UNIT, UNIT)
-    await_all(done_ref.at[:, pl.ds(0, (peers - 1) * group), :], back_send)
-
-
-PREP_A = 2
-CLOSE_A = 2
-PREP_B = 3
-CLOSE_B = 3
-HALO_ORDER = (0, 1)
+        finish(2 + h, edges[1] * CY + h * UNIT, UNIT)
+    await_all(done_ref.at[:, pl.ds(0, (peers - 1) * group), :], load_sem.at[4])
+
+
+PLAN = (
+    ("unit", 0, 0),
+    ("back", 0),
+    ("far", "prep"),
+    ("far", 0),
+    ("unit", 1, 0),
+    ("far", 1),
+    ("back", 1),
+    ("alone", "prep"),
+    ("alone", 0),
+    ("alone", 1),
+    ("unit", 2, 1),
+    ("near", "prep"),
+    ("near", 0),
+    ("back", 2),
+    ("near", 1),
+    ("back", 3),
+    ("unit", 4, 1),
+    ("back", 4),
+    ("back", 5),
+    ("unit", 6, 0),
+    ("back", 6),
+    ("unit", 7, 0),
+    ("back", 7),
+)
 
 
 def body(
@@ -514,8 +560,8 @@
         in_specs=[pl.BlockSpec(memory_space=pl.ANY)] * len(operands),
         out_specs=pl.BlockSpec(memory_space=pltpu.VMEM),
         scratch_shapes=[
-            pltpu.VMEM(flat.shape, jnp.float32),
-            *[pltpu.VMEM(x.shape, x.dtype) for x in operands[1:]],
+            *[pltpu.VMEM(x.shape, x.dtype) for x in operands[:5]],
+            pltpu.VMEM((3, total, total), jnp.int32),
             pltpu.VMEM((quad_rows(total), 4 * total), jnp.bfloat16),
             pltpu.VMEM((2 * total, pair_rows() + total), jnp.bfloat16),
             pltpu.VMEM((layers * group, columns), jnp.float32),
@@ -526,15 +572,12 @@
             pltpu.VMEM((own, total, columns), jnp.float32),
             pltpu.VMEM((own, total, columns), jnp.float32),
             pltpu.VMEM((layers, group, columns), jnp.float32),
-            dma((len(operands),)),
-            dma((2,)),
-            dma((2,)),
+            dma((6,)),
             dma((2,)),
             dma((2, SPLIT)),
             dma,
-            dma((CX * SPLIT, own)),
-            dma,
-            dma((CX - 1 + SPLIT,)),
+            dma((UNITS, own)),
+            dma((CX - 2 + SPLIT,)),
         ],
         compiler_params=pltpu.CompilerParams(collective_id=0, has_side_effects=True),
     )(*operands)

time: 18.6 us -> 18 us (0.968)
  Pallas kernels: 17.6 us -> 17 us
    pallas_call x1, Pallas kernels: 17.6 us -> 17 us  [body(): pl.pallas_call(functools.partial(step_kernel, tiles, peers), out_shape=pl...]
where the time goes in v2:
time: 18 us; the launch traced here: 17.8 us
  Pallas kernels  17 us (94%)
  local copies, waits for them, and re-layouts  0.8 us (4%)
    pallas_call x1, Pallas kernels, body(): pl.pallas_call(functools.partial(step_kernel, tiles, peers), out_shape=pl...  17 us
    unnamed x1, local copies, waits for them, and re-layouts  0.8 us

profile of v2, /device:TPU:25, one launch (start us, length us, event | category | flops | bytes accessed | tf_op | source)
XLA Modules:
  0.0 17.8 jit_solution(17448723393763177483)
XLA Ops:
  0.0 17.0 %shard_map.82 = f32[1024,128]{1,0:T(8,128)S(1)} custom-call(f32[1024,128]{1,0:T(8,128)} %bitcast.14, f32[2,4,2048]{2,1,0:T(4,128)} %speed_hbm.1, s32[1,2048]{1,0:T(1,128)} %bitcast.15, f32[1,16]{1,0:T(1,128)} %bitcast.16, f32[1,64]{1,0:T(1,128)} %bitcast.17, s32[64,64]{1,0:T(8,128)} %levels_hbm.1, s32[64,64]{1,0:T(8,128)} %target_hbm.1, s32[64,64]{1,0:T(8,128)} %weights_hbm.1), custom_call_target="tpu_custom_call" | custom-call | tf_op jit(solution)/shard_map/pallas_call | solution.py:557
  17.0 0.8 %copy.12 = f32[16,4,2048]{2,1,0:T(4,128)} copy(f32[16,4,2048]{2,1,0:T(4,128)S(1)} %bitcast.13) | data formatting | bytes 1048576

commit v3 on v2

--- a/solution.py
+++ b/solution.py
@@ -152,7 +152,6 @@
     target_hbm,
     weights_hbm,
     out_ref,
-    flat_ref,
     speed_ref,
     water_ref,
     settling_ref,
@@ -168,12 +167,15 @@
     whole_ref,
     done_ref,
     back_ref,
+    twin_ref,
+    twin_done_ref,
     load_sem,
     drift_recv,
     halo_recv,
     out_send,
     out_recv,
     back_recv,
+    twin_sem,
 ):
     layers, group, columns = moved_ref.shape
     tile_lanes = columns // LANES
@@ -189,6 +191,9 @@
     else:
         partners = [lax.rem(me + d, peers) for d in range(1, peers)]
 
+    twin = lax.rem(me + peers // 2, peers)
+    beside = peers - 2
+
     barrier = pltpu.get_barrier_semaphore()
 
     @pl.when(has_west)
@@ -203,10 +208,9 @@
         pl.semaphore_signal(barrier, inc=1, device_id={"cls": p}, device_id_type=MESH)
 
     loads = [
-        pltpu.make_async_copy(source, place, load_sem.at[n])
+        pltpu.make_async_copy(source, place, load_sem.at[n + 1])
         for n, (source, place) in enumerate(
             (
-                (flat_hbm, flat_ref),
                 (speed_hbm, speed_ref),
                 (water_hbm, water_ref),
                 (settling_hbm, settling_ref),
@@ -214,10 +218,23 @@
             )
         )
     ]
-    for copy in loads:
+    for copy in loads[:3]:
+        copy.start()
+    for x in range(CX):
+        for j in range(x * (CY // LANES), (x + 1) * (CY // LANES)):
+            for l in range(layers):
+                pltpu.make_async_copy(
+                    flat_hbm.at[:, j * layers + l, 0, :],
+                    field_ref.at[pl.ds(l * group, group), pl.ds(j * LANES, LANES)],
+                    load_sem.at[0 if x < CX - 1 else 6],
+                ).start()
+    for copy in loads[3:]:
         copy.start()
     for n, source in enumerate((levels_hbm, target_hbm, weights_hbm)):
-        pltpu.make_async_copy(source, table_ref.at[n], load_sem.at[len(loads)]).start()
+        pltpu.make_async_copy(source, table_ref.at[n], load_sem.at[len(loads) + 1]).start()
+
+    def await_all(ref, sem):
+        pltpu.make_async_copy(ref, ref, sem).wait()
 
     def span(start, width):
         return pl.ds(pl.multiple_of(start, width), width)
@@ -234,7 +251,7 @@
         def _():
             drift_ref[:, cols(side * (CX + 1))] = jnp.full((layers, CY), LAND, jnp.float32)
 
-    for copy in loads[:4]:
+    for copy in loads[:3]:
         copy.wait()
     drift_ref[:, pl.ds(CY, columns)] = jnp.where(
         jnp.broadcast_to(water_ref[...], (layers, columns)) == 1, speed_ref[0], LAND
@@ -246,13 +263,6 @@
     settle = jnp.sum(jnp.where(diagonal, settling_ref[...], 0.0), axis=1, keepdims=True)
     settle = jnp.broadcast_to(settle, (group, CY))
 
-    def line_up(x):
-        for l in range(layers):
-            for j in range(CY // LANES):
-                field_ref[strip(l), x * CY + j * LANES : x * CY + (j + 1) * LANES] = flat_ref[
-                    pl.ds(x * block + j * layers + l, group, stride=tile_lanes * layers), :
-                ]
-
     def enter():
         before = lax.div(tile + tiles - 1, tiles)
         after = lax.div(2 * (tiles - 1) - tile, tiles)
@@ -301,9 +311,6 @@
                 for h in range(SPLIT):
                     halo(way, h).start()
 
-    def await_all(ref, sem):
-        pltpu.make_async_copy(ref, ref, sem).wait()
-
     def arrival(u):
         inner = (u - SPLIT) // SPLIT + SPLIT
         return u if u < SPLIT else inner if u < (CX - 1) * SPLIT else u - (CX - 2) * (SPLIT - 1)
@@ -327,13 +334,19 @@
         for s in range(own):
             whole_ref[s, span(me * group, group), at] = moved_ref[me * own + s, :, at]
 
-    def backward(n, u, start, width, s):
+    rows = CX - 2
+
+    def slot(k):
+        row = k // SPLIT
+        return row + (k % SPLIT if row == CX - 1 else 0)
+
+    def backward(n, k, start, width, s):
         at = span(start, width)
         return pltpu.make_async_remote_copy(
             src_ref=done_ref.at[s, span(partners[n] * group, group), at],
             dst_ref=back_ref.at[me * own + s, :, at],
-            send_sem=load_sem.at[4],
-            recv_sem=back_recv.at[u],
+            send_sem=twin_sem.at[2] if k // SPLIT == rows - 1 else load_sem.at[4],
+            recv_sem=back_recv.at[slot(k)],
             device_id={"cls": partners[n]},
             device_id_type=MESH,
         )
@@ -381,13 +394,10 @@
                 moved = moved + settle * field_ref[strip(l - 1), cols(x)]
             moved_ref[l, :, cols(x)] = moved
 
-    rows = CX - 2
-
     def prepare(way):
         @pl.when(there(way))
         def _():
-            with jax.named_scope(f'driftwait{way}'):
-                drift(way).wait_recv()
+            drift(way).wait_recv()
 
         transport(edges[way], way)
 
@@ -396,8 +406,7 @@
 
         @pl.when(there(way))
         def _():
-            with jax.named_scope(f'halowait{way}'):
-                halo(way, h).wait_recv()
+            halo(way, h).wait_recv()
             at = pl.ds(h * UNIT, UNIT)
             for l in range(layers):
                 moved_ref[l, :, span(start, UNIT)] += (
@@ -406,22 +415,64 @@
 
         send((rows + way) * SPLIT + h, start, UNIT)
 
+    double = there(0) if peers == 4 else False
+    middle = cols(CX - 2)
+
+    def extra(n, s):
+        return pltpu.make_async_remote_copy(
+            src_ref=moved_ref.at[lax.rem(partners[n] + peers // 2, peers) * own + s, :, middle],
+            dst_ref=twin_ref.at[s, span(me * group, group)],
+            send_sem=twin_sem.at[0],
+            recv_sem=twin_sem.at[1],
+            device_id={"cls": partners[n]},
+            device_id_type=MESH,
+        )
+
+    def send_twice():
+        for s in range(own):
+            for n in range(peers - 1):
+                extra(n, s).start()
+            twin_ref[s, span(me * group, group)] = moved_ref[twin * own + s, :, middle]
+
+    def twin_back(s):
+        return pltpu.make_async_remote_copy(
+            src_ref=twin_done_ref.at[s, span(partners[beside] * group, group)],
+            dst_ref=back_ref.at[twin * own + s, :, middle],
+            send_sem=twin_sem.at[2],
+            recv_sem=back_recv.at[rows - 1],
+            device_id={"cls": partners[beside]},
+            device_id_type=MESH,
+        )
+
+    def twin_unit():
+        await_all(twin_ref.at[:, pl.ds(0, (peers - 1) * group)], twin_sem.at[1])
+        for s in range(own):
+            now = react(twin_ref[s], quad_ref, pair_ref)
+            twin_done_ref[s] = react(now, quad_ref, pair_ref)
+            twin_back(s).start()
+            back_ref[twin * own + s, :, middle] = twin_done_ref[s, span(me * group, group)]
+
     def send_row(x):
         for h in range(SPLIT):
             send((x - 1) * SPLIT + h, x * CY + h * UNIT, UNIT)
 
-    for x in range(CX):
-        line_up(x)
+    inner = pl.ds(0, (CX - 1) * CY)
+    await_all(field_ref.at[:, inner], load_sem.at[0])
     transport(1)
     enter()
+    send_row(1)
+    await_all(field_ref.at[:, cols(CX - 1)], load_sem.at[6])
     reach_out()
-    send_row(1)
     for x in range(2, CX - 1):
         transport(x)
         send_row(x)
 
-    loads[4].wait()
-    await_all(table_ref, load_sem.at[len(loads)])
+    @pl.when(double)
+    def _():
+        send_twice()
+
+    loads[3].wait()
+    await_all(table_ref, load_sem.at[len(loads) + 1])
     build_tables(table_ref.at[0], table_ref.at[1], table_ref.at[2], rate_ref, quad_ref, pair_ref)
 
     @pl.when(jnp.logical_not(there(0)))
@@ -429,10 +480,6 @@
         prepare(0)
         for h in range(SPLIT):
             close(0, h)
-
-    def slot(k):
-        row = k // SPLIT
-        return 0 if row < CX - 2 else row - (CX - 3) + (k % SPLIT if row == CX - 1 else 0)
 
     def unit(u, start, width):
         at = span(start, width)
@@ -449,7 +496,7 @@
     def give_back(k):
         for s in range(own):
             for n in range(peers - 1):
-                backward(n, slot(k), start_of(k), UNIT, s).start()
+                backward(n, k, start_of(k), UNIT, s).start()
 
     def act(name):
         kind, *rest = name
@@ -457,7 +504,19 @@
             k, wide = rest
             unit(k, start_of(k), CY if wide else UNIT)
         elif kind == "back":
-            give_back(rest[0])
+            if rest[0] // SPLIT == rows - 1:
+                pl.when(jnp.logical_not(double))(lambda: give_back(rest[0]))
+            else:
+                give_back(rest[0])
+        elif kind == "beside":
+            @pl.when(double)
+            def _():
+                for s in range(own):
+                    for h in range(SPLIT):
+                        k = (rows - 1) * SPLIT + h
+                        backward(beside, k, start_of(k), UNIT, s).start()
+        elif kind == "twin":
+            pl.when(double)(twin_unit)
         elif kind == "far":
             @pl.when(there(0))
             def _():
@@ -477,13 +536,7 @@
             drift(way).wait_send()
             await_all(halo_ref.at[way], load_sem.at[2 + way])
 
-    def ahead(start, width):
-        return pl.ds(pl.multiple_of(start, UNIT), width)
-
-    def finish(u, start, width):
-        await_all(
-            back_ref.at[pl.ds(0, (peers - 1) * own), :, ahead(start, width)], back_recv.at[u]
-        )
+    def settle_out(start, width):
         for l in range(layers):
             for j in range(width // LANES):
                 at = (lax.div(start, LANES) + j) * layers + l
@@ -491,12 +544,32 @@
                     l, :, span(start + j * LANES, LANES)
                 ]
 
+    def finish(u, start, width):
+        await_all(
+            back_ref.at[pl.ds(0, (peers - 1) * own), :, span(start, width)], back_recv.at[u]
+        )
+        settle_out(start, width)
+
     await_all(moved_ref.at[pl.ds(0, (peers - 1) * own)], out_send)
-    finish(0, CY, rows * CY)
-    finish(1, edges[0] * CY, CY)
+    for q in range(rows - 1):
+        finish(q, (q + 1) * CY, CY)
+
+    @pl.when(double)
+    def _():
+        await_all(twin_ref.at[:, pl.ds(0, (peers - 1) * group)], twin_sem.at[0])
+        await_all(twin_ref.at[:, pl.ds(0, 2 * group)], twin_sem.at[2])
+        await_all(back_ref.at[pl.ds(0, 2 * own), :, middle], back_recv.at[rows - 1])
+
+    @pl.when(jnp.logical_not(double))
+    def _():
+        await_all(done_ref.at[:, pl.ds(0, (peers - 1) * group), middle], twin_sem.at[2])
+        await_all(back_ref.at[pl.ds(0, (peers - 1) * own), :, middle], back_recv.at[rows - 1])
+
+    settle_out((CX - 2) * CY, CY)
+    finish(rows, edges[0] * CY, CY)
     for h in range(SPLIT):
-        finish(2 + h, edges[1] * CY + h * UNIT, UNIT)
-    await_all(done_ref.at[:, pl.ds(0, (peers - 1) * group), :], load_sem.at[4])
+        finish(rows + 1 + h, edges[1] * CY + h * UNIT, UNIT)
+    await_all(done_ref.at[:, pl.ds(0, (peers - 1) * group), pl.ds(0, (CX - 1) * CY)], load_sem.at[4])
 
 
 PLAN = (
@@ -511,11 +584,13 @@
     ("alone", 0),
     ("alone", 1),
     ("unit", 2, 1),
+    ("beside",),
+    ("back", 2),
+    ("back", 3),
     ("near", "prep"),
     ("near", 0),
-    ("back", 2),
+    ("twin",),
     ("near", 1),
-    ("back", 3),
     ("unit", 4, 1),
     ("back", 4),
     ("back", 5),
@@ -542,7 +617,7 @@
     total = kernel_levels.shape[0]
     own = layers // peers
     flat = concentration.reshape(group, layers, columns // LANES, LANES)
-    flat = jnp.transpose(flat, (0, 2, 1, 3)).reshape(-1, LANES)
+    flat = jnp.transpose(flat, (0, 2, 1, 3)).reshape(group, -1, 1, LANES)
     operands = (
         flat,
         velocity,
@@ -560,7 +635,7 @@
         in_specs=[pl.BlockSpec(memory_space=pl.ANY)] * len(operands),
         out_specs=pl.BlockSpec(memory_space=pltpu.VMEM),
         scratch_shapes=[
-            *[pltpu.VMEM(x.shape, x.dtype) for x in operands[:5]],
+            *[pltpu.VMEM(x.shape, x.dtype) for x in operands[1:5]],
             pltpu.VMEM((3, total, total), jnp.int32),
             pltpu.VMEM((quad_rows(total), 4 * total), jnp.bfloat16),
             pltpu.VMEM((2 * total, pair_rows() + total), jnp.bfloat16),
@@ -572,12 +647,15 @@
             pltpu.VMEM((own, total, columns), jnp.float32),
             pltpu.VMEM((own, total, columns), jnp.float32),
             pltpu.VMEM((layers, group, columns), jnp.float32),
-            dma((6,)),
+            pltpu.VMEM((own, total, CY), jnp.float32),
+            pltpu.VMEM((own, total, CY), jnp.float32),
+            dma((7,)),
             dma((2,)),
             dma((2, SPLIT)),
             dma,
             dma((UNITS, own)),
-            dma((CX - 2 + SPLIT,)),
+            dma((CX - 1 + SPLIT,)),
+            dma((3,)),
         ],
         compiler_params=pltpu.CompilerParams(collective_id=0, has_side_effects=True),
     )(*operands)

time: 18 us -> 17.8 us (0.989)
  Pallas kernels: 17 us -> 16.7 us
    pallas_call x1, Pallas kernels: 17 us -> 16.7 us  [body(): pl.pallas_call(functools.partial(step_kernel, tiles, peers), out_shape=pl...]
where the time goes in v3:
time: 17.8 us; the launch traced here: 17.5 us
  Pallas kernels  16.7 us (94%)
  local copies, waits for them, and re-layouts  0.8 us (4%)
    pallas_call x1, Pallas kernels, body(): pl.pallas_call(functools.partial(step_kernel, tiles, peers), out_shape=pl...  16.7 us
    unnamed x1, local copies, waits for them, and re-layouts  0.8 us

profile of v3, /device:TPU:25, one launch (start us, length us, event | category | flops | bytes accessed | tf_op | source)
XLA Modules:
  0.0 17.5 jit_solution(6906748749742040183)
XLA Ops:
  0.0 16.7 %shard_map.82 = f32[1024,128]{1,0:T(8,128)S(1)} custom-call(f32[16,64,1,128]{3,2,1,0:T(1,128)} %bitcast.14, f32[2,4,2048]{2,1,0:T(4,128)} %speed_hbm.1, s32[1,2048]{1,0:T(1,128)} %bitcast.15, f32[1,16]{1,0:T(1,128)} %bitcast.16, f32[1,64]{1,0:T(1,128)} %bitcast.17, s32[64,64]{1,0:T(8,128)} %levels_hbm.1, s32[64,64]{1,0:T(8,128)} %target_hbm.1, ...), custom_call_target="tpu_custom_call" | custom-call | tf_op jit(solution)/shard_map/pallas_call | solution.py:632
  16.7 0.8 %copy.12 = f32[16,4,2048]{2,1,0:T(4,128)} copy(f32[16,4,2048]{2,1,0:T(4,128)S(1)} %bitcast.13) | data formatting | bytes 1048576

commit v4 on v3

--- a/solution.py
+++ b/solution.py
@@ -161,7 +161,6 @@
     pair_ref,
     field_ref,
     drift_ref,
-    outer_ref,
     halo_ref,
     moved_ref,
     whole_ref,
@@ -303,13 +302,13 @@
         )
 
     def reach_out():
-        for way in range(2):
+        for way, h in [(way, h) for h in range(SPLIT) for way in range(2)]:
 
             @pl.when(there(way))
             def _():
-                drift(way).start()
-                for h in range(SPLIT):
-                    halo(way, h).start()
+                if h == 0:
+                    drift(way).start()
+                halo(way, h).start()
 
     def arrival(u):
         inner = (u - SPLIT) // SPLIT + SPLIT
@@ -345,48 +344,43 @@
         return pltpu.make_async_remote_copy(
             src_ref=done_ref.at[s, span(partners[n] * group, group), at],
             dst_ref=back_ref.at[me * own + s, :, at],
-            send_sem=twin_sem.at[2] if k // SPLIT == rows - 1 else load_sem.at[4],
+            send_sem=load_sem.at[5] if k // SPLIT == rows - 1 else load_sem.at[4],
             recv_sem=back_recv.at[slot(k)],
             device_id={"cls": partners[n]},
             device_id_type=MESH,
         )
 
-    def transport(x, way=None):
-        def row(at):
-            value = drift_ref[:, cols(at)]
-            return value, jnp.where(value < 0.5 * LAND, 1.0, 0.0)
-
-        speed, water = row(x + 1)
-        speed_low, water_low = row(x)
-        speed_high, water_high = row(x + 2)
-        face_low = 0.5 * (speed_low + speed) * (water_low * water)
-        face_high = 0.5 * (speed + speed_high) * (water * water_high)
+    def row(at):
+        value = drift_ref[:, at]
+        return value, jnp.where(value < 0.5 * LAND, 1.0, 0.0)
+
+    def face(one, other):
+        return 0.5 * (one[0] + other[0]) * (one[1] * other[1])
+
+    def leaving(flow):
+        return jnp.maximum(flow, 0.0)
+
+    def coming(flow):
+        return -jnp.minimum(flow, 0.0)
+
+    def transport(x, flows):
+        water = row(cols(x + 1))[1]
         v = speed_ref[1, :, cols(x)]
         lane = lax.broadcasted_iota(jnp.int32, v.shape, 1)
-        side_high = 0.5 * (v + pltpu.roll(v, CY - 1, 1)) * (water * pltpu.roll(water, CY - 1, 1))
-        side_high = jnp.where(lane == CY - 1, 0.0, side_high)
-        side_low = pltpu.roll(side_high, 1, 1)
-        up = jnp.maximum
-        down = jnp.minimum
-        centre = (
-            1.0 - up(face_high, 0.0) + down(face_low, 0.0) - up(side_high, 0.0) + down(side_low, 0.0)
-        )
-        west = up(face_low, 0.0)
-        east = -down(face_high, 0.0)
-        south = up(side_low, 0.0)
-        north = -down(side_high, 0.0)
-        if way is None:
-            inner = ((west, x - 1), (east, x + 1))
-        else:
-            eastern = sides[way] == 1
-            outer_ref[way] = jnp.where(eastern, east, west)
-            inner = ((jnp.where(eastern, west, east), x + 1 - 2 * sides[way]),)
+        north = 0.5 * (v + pltpu.roll(v, CY - 1, 1)) * (water * pltpu.roll(water, CY - 1, 1))
+        north = jnp.where(lane == CY - 1, 0.0, north)
+        south = -pltpu.roll(north, 1, 1)
+        centre = 1.0 - leaving(north) - leaving(south)
+        for flow, _ in flows:
+            centre = centre - leaving(flow)
+        from_south, from_north = coming(south), coming(north)
+        inner = [(coming(flow), at) for flow, at in flows]
         for l in range(layers):
             c = field_ref[strip(l), cols(x)]
             moved = (
                 (centre[l : l + 1] - settle) * c
-                + south[l : l + 1] * pltpu.roll(c, 1, 1)
-                + north[l : l + 1] * pltpu.roll(c, CY - 1, 1)
+                + from_south[l : l + 1] * pltpu.roll(c, 1, 1)
+                + from_north[l : l + 1] * pltpu.roll(c, CY - 1, 1)
             )
             for factor, at in inner:
                 moved = moved + factor[l : l + 1] * field_ref[strip(l), cols(at)]
@@ -394,23 +388,33 @@
                 moved = moved + settle * field_ref[strip(l - 1), cols(x)]
             moved_ref[l, :, cols(x)] = moved
 
+    def inner_transport(x):
+        here = row(cols(x + 1))
+        transport(x, [(-face(row(cols(x)), here), x - 1), (face(here, row(cols(x + 2))), x + 1)])
+
     def prepare(way):
+        x = edges[way]
+        inward = 1 - 2 * sides[way]
+        flow = face(row(cols(x + 1)), row(cols(x + 1 + inward))) * inward.astype(jnp.float32)
+        transport(x, [(flow, x + inward)])
+
+    def close(way, h):
+        start = edges[way] * CY + h * UNIT
+
         @pl.when(there(way))
         def _():
-            drift(way).wait_recv()
-
-        transport(edges[way], way)
-
-    def close(way, h):
-        start = edges[way] * CY + h * UNIT
-
-        @pl.when(there(way))
-        def _():
+            if h == 0:
+                drift(way).wait_recv()
             halo(way, h).wait_recv()
-            at = pl.ds(h * UNIT, UNIT)
+            outward = 2 * sides[way] - 1
+            beyond_at = span(sides[way] * (CX + 1) * CY + h * UNIT, UNIT)
+            flow = face(row(span(start + CY, UNIT)), row(beyond_at)) * outward.astype(jnp.float32)
+            out, back = leaving(flow), coming(flow)
+            at = span(start, UNIT)
             for l in range(layers):
-                moved_ref[l, :, span(start, UNIT)] += (
-                    outer_ref[way, l : l + 1, at] * halo_ref[way, strip(l), at]
+                moved_ref[l, :, at] = moved_ref[l, :, at] + (
+                    back[l : l + 1] * halo_ref[way, strip(l), pl.ds(h * UNIT, UNIT)]
+                    - out[l : l + 1] * field_ref[strip(l), at]
                 )
 
         send((rows + way) * SPLIT + h, start, UNIT)
@@ -422,8 +426,8 @@
         return pltpu.make_async_remote_copy(
             src_ref=moved_ref.at[lax.rem(partners[n] + peers // 2, peers) * own + s, :, middle],
             dst_ref=twin_ref.at[s, span(me * group, group)],
-            send_sem=twin_sem.at[0],
-            recv_sem=twin_sem.at[1],
+            send_sem=load_sem.at[6],
+            recv_sem=twin_sem,
             device_id={"cls": partners[n]},
             device_id_type=MESH,
         )
@@ -438,14 +442,14 @@
         return pltpu.make_async_remote_copy(
             src_ref=twin_done_ref.at[s, span(partners[beside] * group, group)],
             dst_ref=back_ref.at[twin * own + s, :, middle],
-            send_sem=twin_sem.at[2],
+            send_sem=load_sem.at[5],
             recv_sem=back_recv.at[rows - 1],
             device_id={"cls": partners[beside]},
             device_id_type=MESH,
         )
 
     def twin_unit():
-        await_all(twin_ref.at[:, pl.ds(0, (peers - 1) * group)], twin_sem.at[1])
+        await_all(twin_ref.at[:, pl.ds(0, (peers - 1) * group)], twin_sem)
         for s in range(own):
             now = react(twin_ref[s], quad_ref, pair_ref)
             twin_done_ref[s] = react(now, quad_ref, pair_ref)
@@ -458,13 +462,13 @@
 
     inner = pl.ds(0, (CX - 1) * CY)
     await_all(field_ref.at[:, inner], load_sem.at[0])
-    transport(1)
+    inner_transport(1)
+    await_all(field_ref.at[:, cols(CX - 1)], load_sem.at[6])
     enter()
+    reach_out()
     send_row(1)
-    await_all(field_ref.at[:, cols(CX - 1)], load_sem.at[6])
-    reach_out()
     for x in range(2, CX - 1):
-        transport(x)
+        inner_transport(x)
         send_row(x)
 
     @pl.when(double)
@@ -475,9 +479,11 @@
     await_all(table_ref, load_sem.at[len(loads) + 1])
     build_tables(table_ref.at[0], table_ref.at[1], table_ref.at[2], rate_ref, quad_ref, pair_ref)
 
+    prepare(0)
+    prepare(1)
+
     @pl.when(jnp.logical_not(there(0)))
     def _():
-        prepare(0)
         for h in range(SPLIT):
             close(0, h)
 
@@ -520,11 +526,11 @@
         elif kind == "far":
             @pl.when(there(0))
             def _():
-                prepare(0) if rest[0] == "prep" else close(0, rest[0])
+                close(0, rest[0])
         else:
             @pl.when(lonely == (1 if kind == "alone" else 0))
             def _():
-                prepare(1) if rest[0] == "prep" else close(1, rest[0])
+                close(1, rest[0])
 
     for name in PLAN:
         act(name)
@@ -556,13 +562,13 @@
 
     @pl.when(double)
     def _():
-        await_all(twin_ref.at[:, pl.ds(0, (peers - 1) * group)], twin_sem.at[0])
-        await_all(twin_ref.at[:, pl.ds(0, 2 * group)], twin_sem.at[2])
+        await_all(twin_ref.at[:, pl.ds(0, (peers - 1) * group)], load_sem.at[6])
+        await_all(twin_ref.at[:, pl.ds(0, 2 * group)], load_sem.at[5])
         await_all(back_ref.at[pl.ds(0, 2 * own), :, middle], back_recv.at[rows - 1])
 
     @pl.when(jnp.logical_not(double))
     def _():
-        await_all(done_ref.at[:, pl.ds(0, (peers - 1) * group), middle], twin_sem.at[2])
+        await_all(done_ref.at[:, pl.ds(0, (peers - 1) * group), middle], load_sem.at[5])
         await_all(back_ref.at[pl.ds(0, (peers - 1) * own), :, middle], back_recv.at[rows - 1])
 
     settle_out((CX - 2) * CY, CY)
@@ -575,19 +581,16 @@
 PLAN = (
     ("unit", 0, 0),
     ("back", 0),
-    ("far", "prep"),
     ("far", 0),
     ("unit", 1, 0),
     ("far", 1),
     ("back", 1),
-    ("alone", "prep"),
     ("alone", 0),
     ("alone", 1),
     ("unit", 2, 1),
     ("beside",),
     ("back", 2),
     ("back", 3),
-    ("near", "prep"),
     ("near", 0),
     ("twin",),
     ("near", 1),
@@ -641,7 +644,6 @@
             pltpu.VMEM((2 * total, pair_rows() + total), jnp.bfloat16),
             pltpu.VMEM((layers * group, columns), jnp.float32),
             pltpu.VMEM((layers, columns + 2 * CY), jnp.float32),
-            pltpu.VMEM((2, layers, CY), jnp.float32),
             pltpu.VMEM((2, layers * group, CY), jnp.float32),
             pltpu.VMEM((layers, group, columns), jnp.float32),
             pltpu.VMEM((own, total, columns), jnp.float32),
@@ -655,7 +657,7 @@
             dma,
             dma((UNITS, own)),
             dma((CX - 1 + SPLIT,)),
-            dma((3,)),
+            dma,
         ],
         compiler_params=pltpu.CompilerParams(collective_id=0, has_side_effects=True),
     )(*operands)

time: 17.8 us -> 17.8 us (level)
  no operation moved by 1% of the time
where the time goes in v4:
time: 17.8 us; the launch traced here: 17.5 us
  Pallas kernels  16.7 us (94%)
  local copies, waits for them, and re-layouts  0.8 us (4%)
    pallas_call x1, Pallas kernels, body(): pl.pallas_call(functools.partial(step_kernel, tiles, peers), out_shape=pl...  16.7 us
    unnamed x1, local copies, waits for them, and re-layouts  0.8 us

profile of v4, /device:TPU:25, one launch (start us, length us, event | category | flops | bytes accessed | tf_op | source)
XLA Modules:
  0.0 17.5 jit_solution(2774128331503666712)
XLA Ops:
  0.0 16.7 %shard_map.82 = f32[1024,128]{1,0:T(8,128)S(1)} custom-call(f32[16,64,1,128]{3,2,1,0:T(1,128)} %bitcast.14, f32[2,4,2048]{2,1,0:T(4,128)} %speed_hbm.1, s32[1,2048]{1,0:T(1,128)} %bitcast.15, f32[1,16]{1,0:T(1,128)} %bitcast.16, f32[1,64]{1,0:T(1,128)} %bitcast.17, s32[64,64]{1,0:T(8,128)} %levels_hbm.1, s32[64,64]{1,0:T(8,128)} %target_hbm.1, ...), custom_call_target="tpu_custom_call" | custom-call | tf_op jit(solution)/shard_map/pallas_call | solution.py:635
  16.7 0.8 %copy.12 = f32[16,4,2048]{2,1,0:T(4,128)} copy(f32[16,4,2048]{2,1,0:T(4,128)S(1)} %bitcast.13) | data formatting | bytes 1048576

commit v5 on v4

--- a/solution.py
+++ b/solution.py
@@ -11,7 +11,7 @@
 CX = 4
 half_scale = 0.5e-05
 STEP = 8
-EDGE = 16
+EDGE = 24
 LARGEST = 448
 LANES = 128
 SPLIT = 2

time: 17.8 us -> 17.8 us (level)
  no operation moved by 1% of the time
where the time goes in v5:
time: 17.8 us; the launch traced here: 17.5 us
  Pallas kernels  16.7 us (94%)
  local copies, waits for them, and re-layouts  0.8 us (4%)
    pallas_call x1, Pallas kernels, body(): pl.pallas_call(functools.partial(step_kernel, tiles, peers), out_shape=pl...  16.7 us
    unnamed x1, local copies, waits for them, and re-layouts  0.8 us

profile of v5, /device:TPU:25, one launch (start us, length us, event | category | flops | bytes accessed | tf_op | source)
XLA Modules:
  0.0 17.5 jit_solution(9755077415832079813)
XLA Ops:
  0.0 16.7 %shard_map.82 = f32[1024,128]{1,0:T(8,128)S(1)} custom-call(f32[16,64,1,128]{3,2,1,0:T(1,128)} %bitcast.14, f32[2,4,2048]{2,1,0:T(4,128)} %speed_hbm.1, s32[1,2048]{1,0:T(1,128)} %bitcast.15, f32[1,16]{1,0:T(1,128)} %bitcast.16, f32[1,64]{1,0:T(1,128)} %bitcast.17, s32[64,64]{1,0:T(8,128)} %levels_hbm.1, s32[64,64]{1,0:T(8,128)} %target_hbm.1, ...), custom_call_target="tpu_custom_call" | custom-call | tf_op jit(solution)/shard_map/pallas_call | solution.py:635
  16.7 0.8 %copy.12 = f32[16,4,2048]{2,1,0:T(4,128)} copy(f32[16,4,2048]{2,1,0:T(4,128)S(1)} %bitcast.13) | data formatting | bytes 1048576
